TPU v7x, 32 devices: a whole 2x2x4 slice. The times are simulated.
32 devices in a mesh: img: 8 (over z, y), sp: 4 (over x, core).
Axes of the slice: x: 2, y: 2, z: 4, core: 2. Of those that a mesh axis runs over, the one named last changes fastest.
Arguments:
- patches: bfloat16 [4096, 1280], P(('img', 'sp')), parts along dimension 0, may hold values from -6 to 6
- pos_ids: int32 [2, 4096], P(None, 'img'), parts along dimension 1, may hold values from 0 to 31, as said below
- norm_gain: float32 [1280], replicated, may hold values from 0.5 to 1.5
- norm_bias: float32 [1280], replicated, may hold values from -3 to 3
- qkv_weight: bfloat16 [1280, 3, 1280], P(None, None, 'sp')
- qkv_bias: float32 [3, 1280], replicated, may hold values from -3 to 3
- proj_weight: bfloat16 [1280, 1280], P('sp'), may hold values from -0.15625 to 0.15625
- proj_bias: float32 [1280], replicated, may hold values from -3 to 3
- merge_gain: float32 [1280], replicated, may hold values from 0.5 to 1.5
- merge_bias: float32 [1280], replicated, may hold values from -3 to 3
- fc1_weight: bfloat16 [5120, 5120], P(None, 'sp'), may hold values from -0.078125 to 0.078125
- fc1_bias: float32 [5120], P('sp'), may hold values from -3 to 3
Outputs:
- vit_out: bfloat16 [4096, 1280], P(('img', 'sp')), parts along dimension 0
- merged_hidden: bfloat16 [1024, 5120], P('img', 'sp'), parts along dimension 0
There are 8 independent parts, one for each index of `img`. A program takes and returns all parts, laid end to end along the dimension named above; an argument that names none is the same for every part. Nothing has to cross between parts.
Inputs may be any that keep to these rules, and one draw needn't show every extreme that they name: pos_ids[0] and pos_ids[1] are the row and column of each patch on a grid of 2 R by 2 C patches, where the grid of 2x2 blocks has R rows and C columns, R C = 128, and one of R and C equals min(8, 128); each aligned run of 4 patches is one 2x2 block in row-major order inside it; every block of the grid appears once, in the order that the argument gives.
All inputs are finite; a program needn't handle non-finite values.
Results may differ from a plain program's by a relative error of at most 0.006.
Values may be sent and summed in bfloat16 or wider, within the bound.
No kernel may reach another device: no remote copies, remote signals or barrier semaphores. Data moves between devices by JAX's collectives and lax.ppermute only.
A program may use at most 64 MiB of HBM per device.

v0:
```python
import jax
import jax.numpy as jnp
from jax import lax
from jax.sharding import PartitionSpec as P

HEADS = 16


def layer_norm(values, gain, bias):
    mean = jnp.mean(values, axis=-1, keepdims=True)
    centered = values - mean
    var = jnp.mean(centered * centered, axis=-1, keepdims=True)
    return centered * lax.rsqrt(var + 1e-06) * gain + bias


def rotate(values, positions, nheads):
    count = values.shape[0]
    hdim = values.shape[1] // nheads
    quarter = hdim // 4
    inv = 1.0 / 10000.0 ** (jnp.arange(quarter, dtype=jnp.float32) * 2.0 / (hdim // 2))
    rows = positions[0].astype(jnp.float32)[:, None] * inv
    cols = positions[1].astype(jnp.float32)[:, None] * inv
    angle = jnp.concatenate([rows, cols, rows, cols], axis=1)
    cosine = jnp.cos(angle)[:, None, :]
    sine = jnp.sin(angle)[:, None, :]
    shaped = values.reshape(count, nheads, hdim)
    half = hdim // 2
    turned = jnp.concatenate([-shaped[..., half:], shaped[..., :half]], axis=-1)
    return (shaped * cosine + turned * sine).reshape(count, nheads * hdim)


def attend(query, keys, value, nheads, hdim):
    count = query.shape[0]
    block = min(512, count)
    qblocks = query.reshape(count // block, block, nheads, hdim)
    kshaped = keys.reshape(count, nheads, hdim)
    vshaped = value.reshape(count, nheads, hdim)
    scale = 1.0 / jnp.sqrt(jnp.float32(hdim))

    def one_block(qpart):
        scores = (
            jnp.einsum("bhd,khd->hbk", qpart, kshaped, preferred_element_type=jnp.float32) * scale
        )
        top = jnp.max(scores, axis=-1, keepdims=True)
        expo = jnp.exp(scores - top)
        weights = (expo / jnp.sum(expo, axis=-1, keepdims=True)).astype(jnp.bfloat16)
        result = jnp.einsum("hbk,khd->bhd", weights, vshaped, preferred_element_type=jnp.float32)
        return result.astype(jnp.bfloat16).reshape(block, nheads * hdim)

    return lax.map(one_block, qblocks).reshape(count, nheads * hdim)


def per_device(
    patches,
    pos_ids,
    norm_gain,
    norm_bias,
    qkv_weight,
    qkv_bias,
    proj_weight,
    proj_bias,
    merge_gain,
    merge_bias,
    fc1_weight,
    fc1_bias,
):
    groups = lax.axis_size("sp")
    where = lax.axis_index("sp")
    prow = patches.shape[0]
    width = patches.shape[1]
    heads_local = HEADS // groups
    hdim = width // HEADS
    local_width = width // groups
    xfloat = patches.astype(jnp.float32)
    normed = layer_norm(xfloat, norm_gain, norm_bias).astype(jnp.bfloat16)
    bias_local = lax.dynamic_slice_in_dim(qkv_bias, where * local_width, local_width, 1)
    qkv = (
        jnp.einsum(
            "pd,dcn->pcn",
            lax.all_gather(normed, "sp", axis=0, tiled=True),
            qkv_weight,
            preferred_element_type=jnp.float32,
        )
        + bias_local[None]
    )
    query = rotate(qkv[:, 0], pos_ids, heads_local).astype(jnp.bfloat16)
    keys = rotate(qkv[:, 1], pos_ids, heads_local).astype(jnp.bfloat16)
    value = qkv[:, 2].astype(jnp.bfloat16)
    spread = jnp.stack([query, keys, value])
    attended = attend(spread[0], spread[1], spread[2], heads_local, hdim)
    returned = lax.all_to_all(attended, "sp", split_axis=0, concat_axis=1, tiled=True)
    projected = jnp.dot(
        returned,
        lax.all_gather(proj_weight, "sp", axis=0, tiled=True),
        preferred_element_type=jnp.float32,
    )
    vit_out = (xfloat + projected + proj_bias).astype(jnp.bfloat16)
    zn = layer_norm(vit_out.astype(jnp.float32), merge_gain, merge_bias).astype(jnp.bfloat16)
    blocks = zn.reshape(prow // 4, 4 * width)
    hidden = (
        jnp.dot(
            lax.all_gather(blocks, "sp", axis=0, tiled=True),
            fc1_weight,
            preferred_element_type=jnp.float32,
        )
        + fc1_bias
    )
    merged_hidden = jax.nn.gelu(hidden, approximate=False).astype(jnp.bfloat16)
    return (vit_out, merged_hidden)


def solution(mesh):
    return jax.shard_map(
        per_device,
        mesh=mesh,
        in_specs=(
            P(("img", "sp"), None),
            P(None, "img"),
            P(),
            P(),
            P(None, None, "sp"),
            P(),
            P("sp", None),
            P(),
            P(),
            P(),
            P(None, "sp"),
            P("sp"),
        ),
        out_specs=(P(("img", "sp"), None), P("img", "sp")),
        check_vma=False,
    )
```

profile of v0, /device:TPU:0, one launch (start us, length us, event | category | flops | bytes accessed | tf_op | source)
XLA Modules:
  0.0 105.2 jit_solution(13298240738997939612)
XLA Ops:
  7.2 0.0 copy-start
  7.2 0.0 all-gather.4.cloned.1.call-start
  7.2 1.2 %convert_reduce_fusion = f32[128]{0:T(128)S(1)} fusion(bf16[128,1280]{1,0:T(8,128)(2,1)} %param.12), kind=kLoop, calls=%fused_computation.17 | loop fusion | flops 327552 | bytes 328192 | tf_op jit(solution)/shard_map/reduce_sum | solution.py:10
  8.5 1.2 %fusion.15 = f32[128]{0:T(128)S(1)} fusion(bf16[128,1280]{1,0:T(8,128)(2,1)} %param.12, f32[128]{0:T(128)S(1)} %broadcast_multiply_fusion.3), kind=kLoop, calls=%fused_computation.24 | loop fusion | flops 655232 | bytes 328704 | tf_op jit(solution)/shard_map/reduce_sum | solution.py:12
  9.7 2.0 %fusion.18 = bf16[128,1280]{1,0:T(8,128)(2,1)} fusion(bf16[128,1280]{1,0:T(8,128)(2,1)} %param.12, f32[1280]{0:T(1024)} %param.15, f32[1280]{0:T(1024)} %param.14, f32[128]{0:T(128)S(1)} %add_rsqrt_fusion.1, f32[128]{0:T(128)S(1)} %broadcast_multiply_fusion.3), kind=kLoop, calls=%fused_computation.27 | loop fusion | flops 983040 | bytes 666624 | tf_op jit(solution)/shard_map/convert_element_type | solution.py:75
  11.7 0.0 all-gather.4.cloned.1.call-update
  11.7 0.0 all-gather.6.cloned.1.call-start
  11.8 0.7 all-gather.6.cloned.1.call-update
  12.5 0.0 all-gather.8.cloned.1.call-start
  12.5 0.8 constant_dynamic-slice_fusion
  13.3 0.8 slice_convert_fusion.2
  14.1 0.1 broadcast_multiply_fusion.1
  14.2 0.6 fusion.40
  14.7 18.0 %all-gather.4.cloned.1.call-done = bf16[512,1280]{1,0:T(8,128)(2,1)} async-done(((bf16[128,1280]{1,0:T(8,128)(2,1)}), bf16[512,1280]{1,0:T(8,128)(2,1)}) %all-gather.4.cloned.1.call-update) | async-done | bytes 1310736 | tf_op jit(solution)/shard_map/all_gather | solution.py:80
  32.8 0.0 copy-done
  32.8 2.8 %convolution_add_fusion.2 = f32[512,3,320]{0,2,1:T(8,128)S(1)} fusion(bf16[1280,3,320]{0,2,1:T(8,128)(2,1)S(1)} %copy-done, bf16[512,1280]{1,0:T(8,128)(2,1)} %all-gather.4.cloned.1.call-done, f32[3,320]{1,0:T(4,128)S(1)} %constant_dynamic-slice_fusion), kind=kOutput, calls=%fused_computation.11 | convolution fusion | flops 1258782720 | bytes 5738240 | tf_op jit(solution)/shard_map/pd,dcn->pcn/dot_general | solution.py:78
  35.5 0.8 slice.51
  36.3 0.1 fusion.42
  36.4 0.1 slice_negate_fusion
  36.6 0.4 fusion.29
  36.9 0.0 copy-start.3
  37.0 3.4 %fusion.43 = (f32[4,512]{1,0:T(4,128)S(1)}, f32[4,512,512]{1,2,0:T(8,128)}) fusion(bf16[512,4,80]{0,2,1:T(8,128)(2,1)S(1)} %get-tuple-element.24, bf16[512,4,80]{0,2,1:T(8,128)(2,1)S(1)} %get-tuple-element.23), kind=kOutput, calls=%fused_computation.75 | convolution fusion | flops 170918400 | bytes 4857856 | tf_op jit(solution)/shard_map/while/body/eval_jaxpr/sub | solution.py:45
  40.4 0.0 copy-done.3
  40.4 0.0 copy-start.1
  40.4 0.0 copy-start.4
  40.4 3.1 %fusion.10 = bf16[512,4,80]{0,2,1:T(8,128)(2,1)S(1)} fusion(bf16[512,4,80]{0,2,1:T(8,128)(2,1)S(1)} %bitcast.30, f32[4,512,512]{1,2,0:T(8,128)} %get-tuple-element.32, f32[4,512]{1,0:T(4,128)S(1)} %get-tuple-element.31), kind=kOutput, calls=%fused_computation.14 | convolution fusion | flops 170033152 | bytes 4857856 | tf_op jit(solution)/shard_map/while/body/eval_jaxpr/hbk,khd->bhd/dot_general | solution.py:47
  43.5 0.0 copy-start.5
  43.5 0.0 copy-start.6
  43.5 0.1 all_to_all.14
  43.6 13.0 %all_to_all.19 = bf16[4,128,320]{1,2,0:T(8,128)(2,1)S(1)} all-to-all(bf16[4,128,320]{1,2,0:T(8,128)(2,1)S(1)} %copy.16), channel_id=1, replica_groups=mesh['img'=8,'sp'=4] {'sp'}, dimensions={0} | all-to-all | bytes 655360 | tf_op jit(solution)/shard_map/all_to_all | solution.py:91
  56.6 0.0 copy-start.7
  56.6 10.5 %all-gather.6.cloned.1.call-done = bf16[1280,1280]{1,0:T(8,128)(2,1)} async-done(((bf16[320,1280]{1,0:T(8,128)(2,1)}), bf16[1280,1280]{1,0:T(8,128)(2,1)}) %all-gather.6.cloned.1.call-update) | async-done | bytes 3276816 | tf_op jit(solution)/shard_map/all_gather | solution.py:94
  67.1 0.0 copy-done.1
  67.1 0.0 copy-done.4
  67.1 2.7 %convert_reduce_fusion.1 = (f32[128]{0:T(128)S(1)}, bf16[128,1280]{1,0:T(8,128)(2,1)S(1)}) fusion(f32[1280]{0:T(1024)S(1)} %copy-done.4, bf16[128,1280]{0,1:T(8,128)(2,1)S(1)} %bitcast.29, bf16[1280,1280]{1,0:T(8,128)(2,1)} %all-gather.6.cloned.1.call-done, bf16[128,1280]{1,0:T(8,128)(2,1)S(1)} %copy-done.1), kind=kOutput, calls=%fused_computation.19 | convolution fusion | flops 420413312 | bytes 4265472 | tf_op jit(solution)/shard_map/dot_general | solution.py:92
  69.8 0.0 copy-start.2
  69.8 0.2 fusion.19
  70.1 0.0 copy-done.5
  70.1 0.0 copy-done.6
  70.1 0.3 fusion.22
  70.4 0.9 reshape.180
  71.3 0.0 all-gather.8.cloned.1.call-update
  71.3 18.3 %all-gather.8.cloned.1.call-done = bf16[128,5120]{1,0:T(8,128)(2,1)} async-done(((bf16[32,5120]{1,0:T(8,128)(2,1)}), bf16[128,5120]{1,0:T(8,128)(2,1)}) %all-gather.8.cloned.1.call-update) | async-done | bytes 1310736 | tf_op jit(solution)/shard_map/all_gather | solution.py:102
  89.6 0.0 copy-done.7
  89.6 9.1 %fusion.25 = bf16[128,1280]{1,0:T(8,128)(2,1)} fusion(bf16[128,5120]{1,0:T(8,128)(2,1)} %all-gather.8.cloned.1.call-done, bf16[5120,1280]{1,0:T(8,128)(2,1)} %param.22, f32[1280]{0:T(1024)S(1)} %copy-done.7), kind=kOutput, calls=%fused_computation.34 | convolution fusion | flops 1688535040 | bytes 14750720 | tf_op jit(solution)/shard_map/dot_general | solution.py:101
  98.7 0.0 copy-done.2
  (6 shorter events, 0.1 us)
Async XLA Ops:
  7.2 25.6 %copy-start = (bf16[1280,3,320]{0,2,1:T(8,128)(2,1)S(1)}, bf16[1280,3,320]{0,2,1:T(8,128)(2,1)}, u32[]{:S(2)}) copy-start(bf16[1280,3,320]{0,2,1:T(8,128)(2,1)} %param.16) | copy-start | bytes 7372804
  7.2 25.6 %all-gather.4.cloned.1.call-start = ((), (), s32[]{:S(2)}) async-start(), calls=%async_computation.1 | async-start | bytes 1638400 | tf_op jit(solution)/shard_map/all_gather | solution.py:80
  11.7 55.4 %all-gather.6.cloned.1.call-start = ((), (), s32[]{:S(2)}) async-start(), calls=%async_computation.2 | async-start | bytes 4096000 | tf_op jit(solution)/shard_map/all_gather | solution.py:94
  12.5 77.2 %all-gather.8.cloned.1.call-start = ((), (), s32[]{:S(2)}) async-start(), calls=%async_computation.3 | async-start | bytes 1638400 | tf_op jit(solution)/shard_map/all_gather | solution.py:102
  36.9 3.5 %copy-start.3 = (bf16[512,1,320]{0,2,1:T(8,128)(2,1)S(1)}, bf16[512,1,320]{0,2,1:T(8,128)(2,1)}, u32[]{:S(2)}) copy-start(bf16[512,1,320]{0,2,1:T(8,128)(2,1)} %slice.51) | copy-start | bytes 983044
  40.4 26.7 %copy-start.1 = (bf16[128,1280]{1,0:T(8,128)(2,1)S(1)}, bf16[128,1280]{1,0:T(8,128)(2,1)}, u32[]{:S(2)}) copy-start(bf16[128,1280]{1,0:T(8,128)(2,1)} %param.12) | copy-start | bytes 983044
  40.4 26.7 %copy-start.4 = (f32[1280]{0:T(1024)S(1)}, f32[1280]{0:T(1024)}, u32[]{:S(2)}) copy-start(f32[1280]{0:T(1024)} %param.19) | copy-start | bytes 15364
  43.5 26.6 %copy-start.5 = (f32[1280]{0:T(1024)S(1)}, f32[1280]{0:T(1024)}, u32[]{:S(2)}) copy-start(f32[1280]{0:T(1024)} %param.21) | copy-start | bytes 15364
  43.5 26.6 %copy-start.6 = (f32[1280]{0:T(1024)S(1)}, f32[1280]{0:T(1024)}, u32[]{:S(2)}) copy-start(f32[1280]{0:T(1024)} %param.20) | copy-start | bytes 15364
  56.6 33.0 %copy-start.7 = (f32[1280]{0:T(1024)S(1)}, f32[1280]{0:T(1024)}, u32[]{:S(2)}) copy-start(f32[1280]{0:T(1024)} %param.23) | copy-start | bytes 15364
  69.8 28.9 %copy-start.2 = (bf16[128,1280]{1,0:T(8,128)(2,1)}, bf16[128,1280]{1,0:T(8,128)(2,1)S(1)}, u32[]{:S(2)}) copy-start(bf16[128,1280]{1,0:T(8,128)(2,1)S(1)} %get-tuple-element.34) | copy-start | bytes 983044
Sparse Core Ops, SparseCore 0:
  11.8 20.8 all-gather.3
  34.3 32.7 all-gather.5
  71.4 18.1 all-gather.7
where the time goes:
time: 106 us; the launch traced here: 105 us
  waiting for transfers between devices  47.5 us (45%)
  matrix products  21 us (20%)
  between operations  13.9 us (13%)
  blocking collectives  13 us (12%)
  other arithmetic  6.95 us (7%)
  local copies, waits for them, and re-layouts  2.74 us (3%)
    all_gather x1, waiting for transfers between devices, per_device(): lax.all_gather(blocks, 'sp', axis=0, tiled=True)  18.3 us
    all_gather x1, waiting for transfers between devices, per_device(): lax.all_gather(normed, 'sp', axis=0, tiled=True)  18 us
    all_to_all x1, blocking collectives, per_device(): lax.all_to_all(attended, 'sp', split_axis=0, concat_axis=1, tiled=True)  13 us
    all_gather x1, waiting for transfers between devices, per_device(): lax.all_gather(proj_weight, 'sp', axis=0, tiled=True)  10.5 us
    dot_general x1, matrix products, per_device(): jnp.dot(lax.all_gather(blocks, 'sp', axis=0, tiled=True), fc1_weight, pre...  9.06 us
    sub x1, matrix products, one_block(): expo = jnp.exp(scores - top)  3.44 us
    dot_general x1, matrix products, one_block(): jnp.einsum('hbk,khd->bhd', weights, vshaped, preferred_element_type=jnp.f...  3.07 us
    dot_general x1, matrix products, per_device(): jnp.einsum('pd,dcn->pcn', lax.all_gather(normed, 'sp', axis=0, tiled=True...  2.77 us
  transfers between devices with their start and end apart: 3, of which 3 were waited for; matrix products, arithmetic and copies ran while one was open for 12% of the time, Pallas kernels for 0%

commit v1 on v0

--- a/solution.py
+++ b/solution.py
@@ -4,6 +4,25 @@
 from jax.sharding import PartitionSpec as P
 
 HEADS = 16
+
+
+def laid_out(blocks, dim):
+    lengths = list(blocks.shape[1:])
+    lengths[dim] *= blocks.shape[0]
+    return jnp.moveaxis(blocks, 0, dim).reshape(lengths)
+
+
+def on_each_block(array, axis, dim, work, out_dim):
+    size, here, rows = (lax.axis_size(axis), lax.axis_index(axis), array.shape[dim])
+    right = [(i, (i + 1) % size) for i in range(size)]
+    blocks = []
+    held = array
+    for turn in range(size):
+        following = held if turn == size - 1 else lax.ppermute(held, axis, right)
+        blocks.append(work(held, (here - turn) % size * rows))
+        held = following
+    blocks = jnp.stack(blocks)[(here - jnp.arange(size)) % size]
+    return laid_out(blocks, out_dim)
 
 
 def layer_norm(values, gain, bias):
@@ -75,11 +94,14 @@
     normed = layer_norm(xfloat, norm_gain, norm_bias).astype(jnp.bfloat16)
     bias_local = lax.dynamic_slice_in_dim(qkv_bias, where * local_width, local_width, 1)
     qkv = (
-        jnp.einsum(
-            "pd,dcn->pcn",
-            lax.all_gather(normed, "sp", axis=0, tiled=True),
-            qkv_weight,
-            preferred_element_type=jnp.float32,
+        on_each_block(
+            normed,
+            "sp",
+            0,
+            lambda shard, start: jnp.einsum(
+                "pd,dcn->pcn", shard, qkv_weight, preferred_element_type=jnp.float32
+            ),
+            0,
         )
         + bias_local[None]
     )

time: 106 us -> 110 us (1.038)
  local copies, waits for them, and re-layouts: 2.74 us -> 6.25 us
  blocking collectives: 13 us -> 10.6 us
  other arithmetic: 6.95 us -> 9.28 us
  starting transfers between devices: 0.12 us -> 2.02 us
  waiting for transfers between devices: 47.5 us -> 46.1 us
    ppermute x0 -> x3, waiting for transfers between devices: none -> 26.3 us  [on_each_block(): following = held if turn == size - 1 else lax.ppermute(held, axis, right)]
    all_gather x1 -> x0, waiting for transfers between devices: 18 us -> none  [per_device(): lax.all_gather(normed, 'sp', axis=0, tiled=True)]
    all_gather x1, waiting for transfers between devices: 10.5 us -> 0.01 us  [per_device(): lax.all_gather(proj_weight, 'sp', axis=0, tiled=True)]
    gather x0 -> x1, local copies, waits for them, and re-layouts: none -> 3.51 us  [on_each_block(): blocks = jnp.stack(blocks)[(here - jnp.arange(size)) % size]]
    all_to_all x1, blocking collectives: 13 us -> 10.6 us  [per_device(): lax.all_to_all(attended, 'sp', split_axis=0, concat_axis=1, tiled=True)]
    ppermute x0 -> x3, starting transfers between devices: none -> 1.94 us  [on_each_block(): following = held if turn == size - 1 else lax.ppermute(held, axis, right)]
    add x0 -> x1, other arithmetic: none -> 1.74 us  [per_device(): on_each_block(normed, 'sp', 0, lambda shard, start: jnp.einsum('pd,dcn->p...]
    another operation x0 -> x1, other arithmetic: none -> 1.46 us  [on_each_block(): blocks = jnp.stack(blocks)[(here - jnp.arange(size)) % size]]
  transfers between devices with their start and end apart: 3 -> 5, of which waited for: 3 -> 4; matrix products, arithmetic and copies ran while one was open for 12% -> 21% of each run, Pallas kernels for 0% -> 0%
where the time goes in v1:
time: 110 us
  waiting for transfers between devices  46.1 us (42%)
  matrix products  21.1 us (19%)
  between operations  14.2 us (13%)
  blocking collectives  10.6 us (10%)
  other arithmetic  9.28 us (8%)
  local copies, waits for them, and re-layouts  6.25 us (6%)
  starting transfers between devices  2.02 us (2%)
    ppermute x3, waiting for transfers between devices, on_each_block(): following = held if turn == size - 1 else lax.ppermute(held, axis, right)  26.3 us
    all_gather x1, waiting for transfers between devices, per_device(): lax.all_gather(blocks, 'sp', axis=0, tiled=True)  19.1 us
    all_to_all x1, blocking collectives, per_device(): lax.all_to_all(attended, 'sp', split_axis=0, concat_axis=1, tiled=True)  10.6 us
    dot_general x1, matrix products, per_device(): jnp.dot(lax.all_gather(blocks, 'sp', axis=0, tiled=True), fc1_weight, pre...  9.06 us
    gather x1, local copies, waits for them, and re-layouts, on_each_block(): blocks = jnp.stack(blocks)[(here - jnp.arange(size)) % size]  3.51 us
    sub x1, matrix products, one_block(): expo = jnp.exp(scores - top)  3.44 us
    dot_general x4, matrix products, per_device(): jnp.einsum('pd,dcn->pcn', shard, qkv_weight, preferred_element_type=jnp.f...  3.18 us
    dot_general x1, matrix products, one_block(): jnp.einsum('hbk,khd->bhd', weights, vshaped, preferred_element_type=jnp.f...  2.73 us
  transfers between devices with their start and end apart: 5, of which 4 were waited for; matrix products, arithmetic and copies ran while one was open for 21% of the time, Pallas kernels for 0%

profile of v1, /device:TPU:0, one launch (start us, length us, event | category | flops | bytes accessed | tf_op | source)
XLA Modules:
  0.0 109.6 jit_solution(10923002193124021199)
XLA Ops:
  7.2 0.0 copy-start
  7.2 0.0 all-gather.3.cloned.1.call-start
  7.2 0.7 all-gather.3.cloned.1.call-update
  7.9 0.0 all-gather.5.cloned.1.call-start
  8.0 1.1 %convert_reduce_fusion = f32[128]{0:T(128)S(1)} fusion(bf16[128,1280]{1,0:T(8,128)(2,1)} %param.12), kind=kLoop, calls=%fused_computation.22 | loop fusion | flops 327552 | bytes 328192 | tf_op jit(solution)/shard_map/reduce_sum | solution.py:29
  9.1 1.2 %fusion.14 = f32[128]{0:T(128)S(1)} fusion(bf16[128,1280]{1,0:T(8,128)(2,1)} %param.12, f32[128]{0:T(128)S(1)} %broadcast_multiply_fusion.3), kind=kLoop, calls=%fused_computation.29 | loop fusion | flops 655232 | bytes 328704 | tf_op jit(solution)/shard_map/reduce_sum | solution.py:31
  10.3 1.3 %fusion.17 = bf16[128,1280]{1,0:T(8,128)(2,1)S(1)} fusion(bf16[128,1280]{1,0:T(8,128)(2,1)} %param.12, f32[1280]{0:T(1024)} %param.15, f32[1280]{0:T(1024)} %param.14, f32[128]{0:T(128)S(1)} %add_rsqrt_fusion.1, f32[128]{0:T(128)S(1)} %broadcast_multiply_fusion.3), kind=kLoop, calls=%fused_computation.32 | loop fusion | flops 983040 | bytes 666624 | tf_op jit(solution)/shard_map/convert_element_type | solution.py:94
  11.6 0.5 collective-permute-start
  12.1 0.8 constant_dynamic-slice_fusion
  12.9 0.8 slice_convert_fusion.2
  13.7 0.1 broadcast_multiply_fusion.1
  13.7 0.6 fusion.43
  14.3 4.4 %collective-permute-done = bf16[128,1280]{1,0:T(8,128)(2,1)S(1)} collective-permute-done((bf16[128,1280]{1,0:T(8,128)(2,1)S(1)}, bf16[128,1280]{1,0:T(8,128)(2,1)S(1)}, u32[]{:S(2)}, u32[]{:S(2)}) %collective-permute-start) | collective-permute-done | bytes 327712 | tf_op jit(solution)/shard_map/ppermute | solution.py:21
  18.8 0.0 collective-permute-start.1
  18.8 0.0 copy-done
  18.8 0.8 convolution_bitcast_fusion.3
  19.6 11.2 %collective-permute-done.1 = bf16[128,1280]{1,0:T(8,128)(2,1)S(1)} collective-permute-done((bf16[128,1280]{1,0:T(8,128)(2,1)S(1)}, bf16[128,1280]{1,0:T(8,128)(2,1)S(1)}, u32[]{:S(2)}, u32[]{:S(2)}) %collective-permute-start.1) | collective-permute-done | bytes 327712 | tf_op jit(solution)/shard_map/ppermute | solution.py:21
  30.8 1.4 %collective-permute-start.2 = (bf16[128,1280]{1,0:T(8,128)(2,1)S(1)}, bf16[128,1280]{1,0:T(8,128)(2,1)S(1)}, u32[]{:S(2)}, u32[]{:S(2)}) collective-permute-start(bf16[128,1280]{1,0:T(8,128)(2,1)S(1)} %collective-permute-done.1), channel_id=1, source_target_pairs={{0,1},{1,2},{2,3},{3,0},{4,5},{5,6},{6,7},{7,4},{8,9},{9,10},{10,1... | collective-permute-start | bytes 983048 | tf_op jit(solution)/shard_map/ppermute | solution.py:21
  32.2 0.8 convolution_bitcast_fusion.2
  33.0 0.8 convolution_bitcast_fusion.1
  33.8 10.7 %collective-permute-done.2 = bf16[128,1280]{1,0:T(8,128)(2,1)S(1)} collective-permute-done((bf16[128,1280]{1,0:T(8,128)(2,1)S(1)}, bf16[128,1280]{1,0:T(8,128)(2,1)S(1)}, u32[]{:S(2)}, u32[]{:S(2)}) %collective-permute-start.2) | collective-permute-done | bytes 327712 | tf_op jit(solution)/shard_map/ppermute | solution.py:21
  44.5 0.8 convolution_bitcast_fusion
  45.3 1.5 %pad_maximum_fusion = f32[4,128,3,320]{1,3,2,0:T(8,128)} fusion(f32[1,128,3,320]{1,3,2,0:T(8,128)S(1)} %convolution_bitcast_fusion, f32[1,128,3,320]{1,3,2,0:T(8,128)S(1)} %convolution_bitcast_fusion.1, f32[1,128,3,320]{1,3,2,0:T(8,128)S(1)} %convolution_bitcast_fusion.2, f32[1,128,3,320]{1,3,2,0:T(8,128)S(1)} %convolution_bitcast_fusion.3), kind=kLoop, calls=%fused_computation.13 | loop fusion | flops 1474560 | bytes 3932160 | tf_op jit(solution)/shard_map/stack | solution.py:24
  46.7 3.5 %gather_fusion = f32[4,128,3,320]{1,3,2,0:T(8,128)} fusion(f32[4,128,3,320]{1,3,2,0:T(8,128)} %pad_maximum_fusion, s32[1024]{0:T(1024)S(1)} %pad_clamp_fusion), kind=kCustom, calls=%fused_computation | custom fusion | bytes 3932176 | tf_op jit(solution)/shard_map/gather | solution.py:24
  50.2 1.7 %bitcast_add_fusion = f32[512,3,320]{0,2,1:T(8,128)S(1)} fusion(f32[3,320]{1,0:T(4,128)S(1)} %constant_dynamic-slice_fusion, f32[4,128,3,320]{1,3,2,0:T(8,128)} %gather_fusion), kind=kLoop, calls=%fused_computation.12 | loop fusion | flops 491520 | bytes 3936000 | tf_op jit(solution)/shard_map/add | solution.py:97
  52.0 0.8 slice.53
  52.8 0.1 fusion.47
  52.8 0.1 slice_negate_fusion
  53.0 0.4 fusion.28
  53.4 0.0 copy-start.3
  53.4 3.4 %fusion.48 = (f32[4,512]{1,0:T(4,128)S(1)}, f32[4,512,512]{1,2,0:T(8,128)}) fusion(bf16[512,4,80]{0,2,1:T(8,128)(2,1)S(1)} %get-tuple-element.24, bf16[512,4,80]{0,2,1:T(8,128)(2,1)S(1)} %get-tuple-element.23), kind=kOutput, calls=%fused_computation.91 | convolution fusion | flops 170918400 | bytes 4857856 | tf_op jit(solution)/shard_map/while/body/eval_jaxpr/sub | solution.py:64
  56.8 0.0 copy-done.3
  56.9 2.7 %fusion.9 = bf16[512,4,80]{0,2,1:T(8,128)(2,1)S(1)} fusion(bf16[512,4,80]{0,2,1:T(8,128)(2,1)S(1)} %bitcast.57, f32[4,512,512]{1,2,0:T(8,128)} %get-tuple-element.32, f32[4,512]{1,0:T(4,128)S(1)} %get-tuple-element.31), kind=kOutput, calls=%fused_computation.19 | convolution fusion | flops 170033152 | bytes 4857856 | tf_op jit(solution)/shard_map/while/body/eval_jaxpr/hbk,khd->bhd/dot_general | solution.py:66
  59.6 0.1 all_to_all.14
  59.7 10.6 %all_to_all.19 = bf16[4,128,320]{1,2,0:T(8,128)(2,1)S(1)} all-to-all(bf16[4,128,320]{1,2,0:T(8,128)(2,1)S(1)} %copy.17), channel_id=1, replica_groups=mesh['img'=8,'sp'=4] {'sp'}, dimensions={0} | all-to-all | bytes 655360 | tf_op jit(solution)/shard_map/all_to_all | solution.py:113
  70.4 0.0 copy-done.1
  70.4 0.0 copy-done.4
  70.4 0.0 copy-start.7
  70.4 2.7 %convert_reduce_fusion.1 = (f32[128]{0:T(128)S(1)}, bf16[128,1280]{1,0:T(8,128)(2,1)S(1)}) fusion(f32[1280]{0:T(1024)S(1)} %copy-done.4, bf16[128,1280]{0,1:T(8,128)(2,1)S(1)} %bitcast.56, bf16[1280,1280]{1,0:T(8,128)(2,1)} %all-gather.3.cloned.1.call-done, bf16[128,1280]{1,0:T(8,128)(2,1)S(1)} %copy-done.1), kind=kOutput, calls=%fused_computation.24 | convolution fusion | flops 420413312 | bytes 4265472 | tf_op jit(solution)/shard_map/dot_general | solution.py:114
  73.1 0.0 copy-start.2
  73.1 0.2 fusion.18
  73.4 0.0 copy-done.5
  73.4 0.0 copy-done.6
  73.4 0.3 fusion.21
  73.6 0.9 reshape.233
  74.6 0.0 all-gather.5.cloned.1.call-update
  74.6 19.1 %all-gather.5.cloned.1.call-done = bf16[128,5120]{1,0:T(8,128)(2,1)} async-done(((bf16[32,5120]{1,0:T(8,128)(2,1)}), bf16[128,5120]{1,0:T(8,128)(2,1)}) %all-gather.5.cloned.1.call-update) | async-done | bytes 1310736 | tf_op jit(solution)/shard_map/all_gather | solution.py:124
  93.7 9.1 %fusion.24 = bf16[128,1280]{1,0:T(8,128)(2,1)} fusion(bf16[128,5120]{1,0:T(8,128)(2,1)} %all-gather.5.cloned.1.call-done, bf16[5120,1280]{1,0:T(8,128)(2,1)} %param.22, f32[1280]{0:T(1024)S(1)} %copy-done.7), kind=kOutput, calls=%fused_computation.39 | convolution fusion | flops 1688535040 | bytes 14750720 | tf_op jit(solution)/shard_map/dot_general | solution.py:123
  (15 shorter events, 0.1 us)
Async XLA Ops:
  7.2 11.6 %copy-start = (bf16[1280,3,320]{0,2,1:T(8,128)(2,1)S(1)}, bf16[1280,3,320]{0,2,1:T(8,128)(2,1)}, u32[]{:S(2)}) copy-start(bf16[1280,3,320]{0,2,1:T(8,128)(2,1)} %param.16) | copy-start | bytes 7372804
  7.2 63.2 %all-gather.3.cloned.1.call-start = ((), (), s32[]{:S(2)}) async-start(), calls=%async_computation.1 | async-start | bytes 4096000 | tf_op jit(solution)/shard_map/all_gather | solution.py:116
  7.9 85.8 %all-gather.5.cloned.1.call-start = ((), (), s32[]{:S(2)}) async-start(), calls=%async_computation.2 | async-start | bytes 1638400 | tf_op jit(solution)/shard_map/all_gather | solution.py:124
  11.6 7.2 %collective-permute-start = (bf16[128,1280]{1,0:T(8,128)(2,1)S(1)}, bf16[128,1280]{1,0:T(8,128)(2,1)S(1)}, u32[]{:S(2)}, u32[]{:S(2)}) collective-permute-start(bf16[128,1280]{1,0:T(8,128)(2,1)S(1)} %fusion.17), channel_id=1, source_target_pairs={{0,1},{1,2},{2,3},{3,0},{4,5},{5,6},{6,7},{7,4},{8,9},{9,10},{10,1... | collective-permute-start | bytes 983048 | tf_op jit(solution)/shard_map/ppermute | solution.py:21
  18.8 12.1 %collective-permute-start.1 = (bf16[128,1280]{1,0:T(8,128)(2,1)S(1)}, bf16[128,1280]{1,0:T(8,128)(2,1)S(1)}, u32[]{:S(2)}, u32[]{:S(2)}) collective-permute-start(bf16[128,1280]{1,0:T(8,128)(2,1)S(1)} %collective-permute-done), channel_id=1, source_target_pairs={{0,1},{1,2},{2,3},{3,0},{4,5},{5,6},{6,7},{7,4},{8,9},{9,10},{10,1... | collective-permute-start | bytes 983048 | tf_op jit(solution)/shard_map/ppermute | solution.py:21
  30.8 13.6 %collective-permute-start.2 = (bf16[128,1280]{1,0:T(8,128)(2,1)S(1)}, bf16[128,1280]{1,0:T(8,128)(2,1)S(1)}, u32[]{:S(2)}, u32[]{:S(2)}) collective-permute-start(bf16[128,1280]{1,0:T(8,128)(2,1)S(1)} %collective-permute-done.1), channel_id=1, source_target_pairs={{0,1},{1,2},{2,3},{3,0},{4,5},{5,6},{6,7},{7,4},{8,9},{9,10},{10,1... | collective-permute-start | bytes 983048 | tf_op jit(solution)/shard_map/ppermute | solution.py:21
  53.4 3.5 %copy-start.3 = (bf16[512,1,320]{0,2,1:T(8,128)(2,1)S(1)}, bf16[512,1,320]{0,2,1:T(8,128)(2,1)}, u32[]{:S(2)}) copy-start(bf16[512,1,320]{0,2,1:T(8,128)(2,1)} %slice.53) | copy-start | bytes 983044
  56.8 13.5 %copy-start.1 = (bf16[128,1280]{1,0:T(8,128)(2,1)S(1)}, bf16[128,1280]{1,0:T(8,128)(2,1)}, u32[]{:S(2)}) copy-start(bf16[128,1280]{1,0:T(8,128)(2,1)} %param.12) | copy-start | bytes 983044
  56.8 13.5 %copy-start.4 = (f32[1280]{0:T(1024)S(1)}, f32[1280]{0:T(1024)}, u32[]{:S(2)}) copy-start(f32[1280]{0:T(1024)} %param.19) | copy-start | bytes 15364
  70.3 3.0 %copy-start.5 = (f32[1280]{0:T(1024)S(1)}, f32[1280]{0:T(1024)}, u32[]{:S(2)}) copy-start(f32[1280]{0:T(1024)} %param.21) | copy-start | bytes 15364
  70.4 3.0 %copy-start.6 = (f32[1280]{0:T(1024)S(1)}, f32[1280]{0:T(1024)}, u32[]{:S(2)}) copy-start(f32[1280]{0:T(1024)} %param.20) | copy-start | bytes 15364
  70.4 23.3 %copy-start.7 = (f32[1280]{0:T(1024)S(1)}, f32[1280]{0:T(1024)}, u32[]{:S(2)}) copy-start(f32[1280]{0:T(1024)} %param.23) | copy-start | bytes 15364
  73.1 29.7 %copy-start.2 = (bf16[128,1280]{1,0:T(8,128)(2,1)}, bf16[128,1280]{1,0:T(8,128)(2,1)S(1)}, u32[]{:S(2)}) copy-start(bf16[128,1280]{1,0:T(8,128)(2,1)S(1)} %get-tuple-element.34) | copy-start | bytes 983044
Sparse Core Ops, SparseCore 0:
  9.5 38.3 all-gather.2
  74.7 18.9 all-gather.4
